TPU v7x, 32 devices: a whole 2x2x4 slice. The times are simulated.
32 devices in a mesh: groups: 2 (over y), az: 4 (over z), rg: 2 (over x), acq: 2 (over core).
Axes of the slice: x: 2, y: 2, z: 4, core: 2. Of those that a mesh axis runs over, the one named last changes fastest.
Arguments:
- image_stack: bfloat16 [2, 64, 32, 4, 256], P(None, ('az', 'acq'), 'groups', 'rg'), parts along dimension 2, may hold values from -12 to 12
- steering: bfloat16 [4, 2, 64, 512], P('rg'), as said below
- wiener_filter: bfloat16 [4, 2, 64, 64], P('rg'), may hold values from -0.5 to 0.5
- range_group: int32 [4], P('rg'), may hold values from 0 to 3, as said below
- lay_list: int32 [32, 4, 32], P(('groups', 'az', 'acq'), 'rg'), parts along dimension 0, may hold values from 0 to 255, as said below
- lay_count: int32 [32, 4], P(('groups', 'az', 'acq'), 'rg'), parts along dimension 0, may hold values from 0 to 32, as said below
Outputs:
- power: bfloat16 [32, 4, 512, 256], P(('groups', 'az', 'acq'), 'rg'), parts along dimension 0
There are 2 independent parts, one for each index of `groups`. A program takes and returns all parts, laid end to end along the dimension named above; an argument that names none is the same for every part. Nothing has to cross between parts.
Inputs may be any that keep to these rules, and one draw needn't show every extreme that they name: `lay_list`: within one block the 32 entries are distinct pixels. The first lay_count entries of a block's list are its layover pixels; some block has 32. `range_group`: range block r belongs to a group from (r // 2) * 2 to (r // 2) * 2 + 1. `steering`: every complex entry has modulus 1 / sqrt(512) up to rounding.
All inputs are finite; a program needn't handle non-finite values.
Results may differ from a plain program's by a relative error of at most 0.0075.
Values may be sent and summed in bfloat16 or wider, within the bound.
No kernel may reach another device: no remote copies, remote signals or barrier semaphores. Data moves between devices by JAX's collectives and lax.ppermute only.
A program may use at most 64 MiB of HBM per device.

v0:
```python
import jax
import jax.numpy as jnp
from jax import lax
from jax.sharding import PartitionSpec as P

K = 64
E = 512
LMAX = 32
GRP_DEV = 2
ITERS = 8
STEP_SIZE = 0.5
SHRINK = 0.25
block_rows = 32


def complex_block(complex_parts):
    real_part = complex_parts[0]
    imag_part = complex_parts[1]
    upper = jnp.concatenate([real_part, -imag_part], axis=1)
    lower = jnp.concatenate([imag_part, real_part], axis=1)
    return jnp.concatenate([upper, lower], axis=0)


def ista_power(lane_data, operator):
    target = lane_data.astype(jnp.float32)
    elevation = operator.shape[1] // 2

    def sweep(sweep_index, estimate):
        rounded = estimate.astype(jnp.bfloat16)
        predicted = jnp.dot(rounded, operator.T, preferred_element_type=jnp.float32)
        misfit = (target - predicted).astype(jnp.bfloat16)
        update = estimate + STEP_SIZE * jnp.dot(
            misfit, operator, preferred_element_type=jnp.float32
        )
        magnitude = update[:, :elevation] ** 2 + update[:, elevation:] ** 2
        factor = jnp.maximum(1.0 - SHRINK * lax.rsqrt(jnp.maximum(magnitude, SHRINK * SHRINK)), 0.0)
        return update * jnp.concatenate([factor, factor], axis=1)

    start = jnp.zeros((lane_data.shape[0], 2 * elevation), jnp.float32)
    estimate = lax.fori_loop(0, ITERS, sweep, start)
    return (estimate[:, :elevation] ** 2 + estimate[:, elevation:] ** 2).astype(jnp.bfloat16)


def pack_order(usable):
    live_flags = usable.astype(jnp.int32)
    live_total = jnp.sum(live_flags)
    before_live = jnp.cumsum(live_flags) - live_flags
    before_empty = jnp.cumsum(1 - live_flags) - (1 - live_flags)
    lane_slot = jnp.where(usable, before_live, live_total + before_empty)
    source = (
        jnp.zeros_like(lane_slot).at[lane_slot].set(jnp.arange(lane_slot.shape[0], dtype=jnp.int32))
    )
    return (lane_slot, source, live_total)


def solve_lanes(lane_data, usable, operator):
    lane_slot, source, live_total = pack_order(usable)
    packed = jnp.take(lane_data, source, axis=0)
    lane_total = lane_data.shape[0]
    elevation = operator.shape[1] // 2

    def one_block(block_turn, result):
        row_block = lax.dynamic_slice_in_dim(packed, block_turn * block_rows, block_rows, 0)
        return lax.dynamic_update_slice_in_dim(
            result, ista_power(row_block, operator), block_turn * block_rows, 0
        )

    turns = (live_total + block_rows - 1) // block_rows
    result = lax.fori_loop(0, turns, one_block, jnp.zeros((lane_total, elevation), jnp.bfloat16))
    return jnp.take(result, lane_slot, axis=0)


def shards(image_stack, steering, wiener_filter, range_group, lay_list, lay_count):
    halves, acq_share, azb_all, range_local, block_pixels = image_stack.shape
    relaid = lax.all_to_all(
        image_stack.reshape(halves, 1, acq_share, azb_all, range_local, block_pixels),
        ("az", "acq"),
        split_axis=3,
        concat_axis=1,
        tiled=True,
    )
    blocks = lay_list.shape[0]
    pixels = relaid.reshape(2 * K, blocks, range_local, block_pixels)
    first_group = lax.axis_index("rg") * GRP_DEV
    operators = []
    wiener_sets = []
    lane_sets = []
    usable_sets = []
    chosen_sets = []
    for column in range(range_local):
        pick_group = jnp.arange(GRP_DEV, dtype=jnp.int32) == range_group[column] - first_group
        steer_parts = jnp.sum(
            jnp.where(pick_group[:, None, None, None], steering, jnp.zeros_like(steering)), axis=0
        )
        filter_parts = jnp.sum(
            jnp.where(
                pick_group[:, None, None, None], wiener_filter, jnp.zeros_like(wiener_filter)
            ),
            axis=0,
        )
        operator = complex_block(steer_parts)
        filter_matrix = complex_block(filter_parts)
        block_data = pixels[:, :, column, :]
        filtered = jnp.einsum(
            "ij,jap->iap", filter_matrix, block_data, preferred_element_type=jnp.float32
        ).astype(jnp.bfloat16)
        beamed = jnp.einsum("ie,iap->aep", operator, filtered, preferred_element_type=jnp.float32)
        wiener_sets.append(beamed[:, :E] ** 2 + beamed[:, E:] ** 2)
        listed = lay_list[:, column, :]
        live_count = lay_count[:, column]
        usable = jnp.arange(LMAX, dtype=jnp.int32)[None, :] < live_count[:, None]
        chosen = (
            (listed[:, :, None] == jnp.arange(block_pixels, dtype=jnp.int32)[None, None, :])
            & usable[:, :, None]
        ).astype(jnp.bfloat16)
        lane_data = jnp.einsum(
            "alp,iap->ali", chosen, block_data, preferred_element_type=jnp.float32
        ).astype(jnp.bfloat16)
        operators.append(operator)
        lane_sets.append(lane_data.reshape(blocks * LMAX, 2 * K))
        usable_sets.append(usable.reshape(blocks * LMAX))
        chosen_sets.append(chosen)
    powers = [
        solve_lanes(lane_sets[column], usable_sets[column], operators[column])
        for column in range(range_local)
    ]
    outputs = []
    for column in range(range_local):
        lay_power = powers[column].reshape(blocks, LMAX, E)
        placed = jnp.einsum(
            "alp,ale->aep", chosen_sets[column], lay_power, preferred_element_type=jnp.float32
        )
        covered = jnp.sum(chosen_sets[column].astype(jnp.float32), axis=1)
        outputs.append(
            jnp.where(covered[:, None, :] > 0.5, placed, wiener_sets[column]).astype(jnp.bfloat16)
        )
    return jnp.stack(outputs, axis=1)


def solution(mesh):
    return jax.shard_map(
        shards,
        mesh=mesh,
        in_specs=(
            P(None, ("az", "acq"), "groups", "rg", None),
            P("rg", None, None, None),
            P("rg", None, None, None),
            P("rg"),
            P(("groups", "az", "acq"), "rg", None),
            P(("groups", "az", "acq"), "rg"),
        ),
        out_specs=P(("groups", "az", "acq"), "rg", None, None),
        check_vma=False,
    )
```

profile of v0, /device:TPU:27, one launch (start us, length us, event | category | flops | bytes accessed | tf_op | source)
XLA Modules:
  0.0 42.8 jit_solution(8267527143187497523)
XLA Ops:
  0.0 1.9 %copy.39 = bf16[2,8,16,2,256]{4,3,1,0,2:T(2,128)(2,1)} copy(bf16[2,8,16,2,256]{4,3,2,1,0:T(2,128)(2,1)} %param.18) | data formatting | bytes 524288 | tf_op args[0]
  1.9 5.4 %all-to-all-start = ((bf16[2,1,8,16,2,256]{5,4,2,0,1,3:T(2,128)(2,1)}), bf16[2,1,8,16,2,256]{5,4,2,0,1,3:T(2,128)(2,1)S(1)}, u32[]{:S(2)}, u32[]{:S(2)}) async-start(bf16[2,1,8,16,2,256]{5,4,2,0,1,3:T(2,128)(2,1)} %bitcast.76), calls=%async_computation | async-start | bytes 524288 | tf_op jit(solution)/shard_map/all_to_all | solution.py:75
  7.3 1.0 %slice_reduce_fusion.1 = (s32[2]{0:T(128)S(1)}, s32[2]{0:T(128)S(1)}) fusion(s32[2,2]{1,0:T(2,128)} %param.23), kind=kLoop, calls=%fused_computation.142 | loop fusion | bytes 32 | tf_op jit(solution)/shard_map/slice | solution.py:110
  8.3 0.7 %convert_reduce_fusion.3 = s32[]{:T(128)} fusion(s32[2]{0:T(128)S(1)} %get-tuple-element.175), kind=kLoop, calls=%fused_computation.139 | loop fusion | flops 191 | bytes 12 | tf_op jit(solution)/shard_map/reduce_sum | solution.py:46
  9.4 0.8 %convert_reduce_fusion.2 = s32[]{:T(128)} fusion(s32[2]{0:T(128)S(1)} %get-tuple-element.176), kind=kLoop, calls=%fused_computation.136 | loop fusion | flops 191 | bytes 12 | tf_op jit(solution)/shard_map/reduce_sum | solution.py:46
  10.6 1.4 %fusion.92 = (s32[64]{0:T(128)S(1)}, s32[64]{0:T(128)S(1)}, s32[64]{0:T(128)S(1)}, s32[64]{0:T(128)S(1)}, s32[64]{0:T(128)S(1)}, /*index=5*/s32[64]{0:T(128)S(1)}) fusion(s32[64,1]{1,0:T(8,128)S(1)} %reduce-window.14, pred[64,1]{1,0:T(8,128)(4,1)S(1)} %lt.160, s32[64,1]{1,0:T(8,128)S(1)} %reduce-window.15, s32[]{:T(128)} %convert_reduce_fusion.3, ...), kind=kLoop, calls=%fused_computation.156 | loop fusion | flops 1152 | bytes 2696 | tf_op jit(solution)/shard_map/reduce-window
  12.0 0.8 %scatter_custom_fusion = s32[64]{0:T(128)S(1)} fusion(s32[64]{0:T(128)S(1)} %get-tuple-element.170, s32[64]{0:T(128)S(1)} %iota.35, s32[]{:T(128)} %constant.130.clone.1), kind=kCustom, calls=%fused_computation.148 | custom fusion | bytes 260 | tf_op jit(solution)/shard_map/scatter | solution.py:51
  12.8 1.3 %fusion.95 = (s32[1]{0:T(128)}, s32[1]{0:T(128)}) fusion(s32[2]{0:T(128)} %param.21), kind=kLoop, calls=%fused_computation.159 | loop fusion | bytes 16 | tf_op jit(solution)/shard_map/slice | solution.py:91
  15.5 1.1 %select_reduce_fusion.1 = (bf16[2,64,512]{2,1,0:T(8,128)(2,1)S(1)}, bf16[2,64,512]{2,1,0:T(8,128)(2,1)S(1)}) fusion(bf16[2,2,64,512]{3,2,1,0:T(8,128)(2,1)} %param.19, pred[2]{0:T(512)(128)(4,1)S(1)} %iota_compare_fusion.5, pred[2]{0:T(512)(128)(4,1)S(1)} %iota_compare_fusion.4), kind=kLoop, calls=%fused_computation.71 | loop fusion | flops 393216 | bytes 524292 | tf_op jit(solution)/shard_map/reduce_sum | solution.py:92
  16.7 0.8 %scatter_custom_fusion.1 = s32[64]{0:T(128)S(1)} fusion(s32[64]{0:T(128)S(1)} %get-tuple-element.230, s32[64]{0:T(128)S(1)} %iota.37, s32[]{:T(128)} %constant.130.clone.1), kind=kCustom, calls=%fused_computation.146 | custom fusion | bytes 260 | tf_op jit(solution)/shard_map/scatter | solution.py:51
  17.7 0.6 %compare_and_fusion.2 = (pred[64]{0:T(512)(128)(4,1)S(1)}, s32[64]{0:T(128)S(1)}) fusion(pred[64]{0:T(512)(128)(4,1)S(1)} %lt.139, s32[64]{0:T(128)S(1)} %get-tuple-element.171, s32[]{:T(128)} %convert_reduce_fusion.3, s32[64]{0:T(128)S(1)} %get-tuple-element.169), kind=kLoop, calls=%fused_computation.134 | loop fusion | flops 768 | bytes 900 | tf_op jit(solution)/shard_map/jit(_take)/and | solution.py:70
  18.6 0.7 %compare_and_fusion = (pred[64]{0:T(512)(128)(4,1)S(1)}, s32[64]{0:T(128)S(1)}) fusion(pred[64]{0:T(512)(128)(4,1)S(1)} %lt.145, s32[64]{0:T(128)S(1)} %get-tuple-element.229, s32[]{:T(128)} %convert_reduce_fusion.2, s32[64]{0:T(128)S(1)} %get-tuple-element.231), kind=kLoop, calls=%fused_computation.132 | loop fusion | flops 768 | bytes 900 | tf_op jit(solution)/shard_map/jit(_take)/and | solution.py:70
  21.1 0.6 %gather_fusion = bf16[64,128]{1,0:T(8,128)(2,1)S(1)} fusion(bf16[64,128]{1,0:T(8,128)(2,1)S(1)} %bitcast.90, s32[1024]{0:T(1024)S(1)} %pad_clamp_fusion.3), kind=kCustom, calls=%fused_computation.clone | custom fusion | bytes 33024 | tf_op jit(solution)/shard_map/jit(_take)/gather | solution.py:58
  21.9 7.7 %while.47 = (s32[]{:T(128)}, bf16[64,512]{1,0:T(8,128)(2,1)S(1)}, s32[]{:T(128)}, bf16[64,128]{1,0:T(8,128)(2,1)S(1)}, bf16[128,1024]{1,0:T(8,128)(2,1)S(1)}, /*...) while((s32[]{:T(128)}, bf16[64,512]{1,0:T(8,128)(2,1)S(1)}, ...), condition=%wide.region_9.11_spmd, body=%wide.region_6.10_spmd.sunk | while | flops 17199112 | bytes 1253674 | solution.py:69
  21.9 3.8 %while.50 = (s32[]{:T(128)}, f32[32,1024]{1,0:T(8,128)S(1)}, bf16[128,1024]{1,0:T(8,128)(2,1)S(1)}, f32[32,128]{1,0:T(8,128)S(1)}, s32[]{:T(128)}, /*index=5*/s32[]{:T(128)}) while((s32[]{:T(128)}, f32[32,1024]{1,0:T(8,128)S(1)}, bf16[128,1024]{1,0:T(8,128)(2,1)S(1)}, f32[32,128]{1,0:T(8,128)S(1)}, s32[]{:T(128)}, ...), condition=%wide.region_8.9_spmd.clone, body=%wide.region_7.8_spmd.clone.sunk | while | flops 17129476 | bytes 1065039 | solution.py:40
  21.9 0.4 fusion.120
  22.4 0.4 fusion.120
  23.4 0.4 fusion.120
  23.8 0.4 fusion.120
  24.3 0.4 fusion.120
  25.2 0.4 fusion.120
  25.8 3.8 %while.50 = (s32[]{:T(128)}, f32[32,1024]{1,0:T(8,128)S(1)}, bf16[128,1024]{1,0:T(8,128)(2,1)S(1)}, f32[32,128]{1,0:T(8,128)S(1)}, s32[]{:T(128)}, /*index=5*/s32[]{:T(128)}) while((s32[]{:T(128)}, f32[32,1024]{1,0:T(8,128)S(1)}, bf16[128,1024]{1,0:T(8,128)(2,1)S(1)}, f32[32,128]{1,0:T(8,128)S(1)}, s32[]{:T(128)}, ...), condition=%wide.region_8.9_spmd.clone, body=%wide.region_7.8_spmd.clone.sunk | while | flops 17129476 | bytes 1065039 | solution.py:40
  26.7 0.4 fusion.120
  29.6 0.6 %gather_fusion.2 = bf16[64,128]{1,0:T(8,128)(2,1)S(1)} fusion(bf16[64,128]{1,0:T(8,128)(2,1)S(1)} %bitcast.89, s32[1024]{0:T(1024)S(1)} %pad_clamp_fusion.1), kind=kCustom, calls=%fused_computation.2.clone | custom fusion | bytes 33024 | tf_op jit(solution)/shard_map/jit(_take)/gather | solution.py:58
  30.3 7.7 %while.49 = (s32[]{:T(128)}, bf16[64,512]{1,0:T(8,128)(2,1)S(1)}, s32[]{:T(128)}, bf16[64,128]{1,0:T(8,128)(2,1)S(1)}, bf16[128,1024]{1,0:T(8,128)(2,1)S(1)}, /*...) while((s32[]{:T(128)}, bf16[64,512]{1,0:T(8,128)(2,1)S(1)}, ...), condition=%wide.region_20.23_spmd, body=%wide.region_17.22_spmd.sunk | while | flops 17199112 | bytes 1253674 | solution.py:69
  30.4 3.8 %while.51 = (s32[]{:T(128)}, f32[32,1024]{1,0:T(8,128)S(1)}, bf16[128,1024]{1,0:T(8,128)(2,1)S(1)}, f32[32,128]{1,0:T(8,128)S(1)}, s32[]{:T(128)}, /*index=5*/s32[]{:T(128)}) while((s32[]{:T(128)}, f32[32,1024]{1,0:T(8,128)S(1)}, bf16[128,1024]{1,0:T(8,128)(2,1)S(1)}, f32[32,128]{1,0:T(8,128)S(1)}, s32[]{:T(128)}, ...), condition=%wide.region_19.21_spmd.clone, body=%wide.region_18.20_spmd.clone.sunk | while | flops 17129476 | bytes 1065039 | solution.py:40
  34.2 3.8 %while.51 = (s32[]{:T(128)}, f32[32,1024]{1,0:T(8,128)S(1)}, bf16[128,1024]{1,0:T(8,128)(2,1)S(1)}, f32[32,128]{1,0:T(8,128)S(1)}, s32[]{:T(128)}, /*index=5*/s32[]{:T(128)}) while((s32[]{:T(128)}, f32[32,1024]{1,0:T(8,128)S(1)}, bf16[128,1024]{1,0:T(8,128)(2,1)S(1)}, f32[32,128]{1,0:T(8,128)S(1)}, s32[]{:T(128)}, ...), condition=%wide.region_19.21_spmd.clone, body=%wide.region_18.20_spmd.clone.sunk | while | flops 17129476 | bytes 1065039 | solution.py:40
  38.1 0.7 %gather_fusion.1 = bf16[64,512]{1,0:T(8,128)(2,1)S(1)} fusion(bf16[64,512]{1,0:T(8,128)(2,1)S(1)} %get-tuple-element.133, s32[1024]{0:T(1024)S(1)} %pad_clamp_fusion.2), kind=kCustom, calls=%fused_computation.1.clone | custom fusion | bytes 131328 | tf_op jit(solution)/shard_map/jit(_take)/gather | solution.py:70
  38.8 0.7 %gather_fusion.3 = bf16[64,512]{1,0:T(8,128)(2,1)S(1)} fusion(bf16[64,512]{1,0:T(8,128)(2,1)S(1)} %get-tuple-element.134, s32[1024]{0:T(1024)S(1)} %pad_clamp_fusion), kind=kCustom, calls=%fused_computation.3.clone | custom fusion | bytes 131328 | tf_op jit(solution)/shard_map/jit(_take)/gather | solution.py:70
  39.6 0.6 %convolution_bitcast_fusion.1 = f32[2,1024,256]{2,1,0:T(8,128)S(1)} fusion(bf16[128,2,2,256]{3,0,1,2:T(8,128)(2,1)S(1)} %bitcast.87, bf16[64,64]{1,0:T(8,128)(2,1)S(1)} %get-tuple-element.236, bf16[64,64]{1,0:T(8,128)(2,1)S(1)} %get-tuple-element.237, bf16[64,64]{1,0:T(8,128)(2,1)S(1)} %get-tuple-element.238, bf16[64,512]{1,0:T(8,128)(2,1)S(1)} %get-tuple-element.232, ...), kind=kOutput, calls=%fused_computation.47 | convolution fusion | flops 152240128 | bytes 2473984 | tf_op jit(solution)/shard_map/ie,iap->aep/dot_general | solution.py:107
  40.7 0.6 %convolution_bitcast_fusion = f32[2,1024,256]{2,1,0:T(8,128)S(1)} fusion(bf16[128,2,2,256]{3,0,1,2:T(8,128)(2,1)S(1)} %bitcast.88, bf16[64,64]{1,0:T(8,128)(2,1)S(1)} %get-tuple-element.224, bf16[64,64]{1,0:T(8,128)(2,1)S(1)} %get-tuple-element.223, bf16[64,64]{1,0:T(8,128)(2,1)S(1)} %get-tuple-element.239, bf16[64,512]{1,0:T(8,128)(2,1)S(1)} %get-tuple-element.220, ...), kind=kOutput, calls=%fused_computation.46 | convolution fusion | flops 152240128 | bytes 2473984 | tf_op jit(solution)/shard_map/ie,iap->aep/dot_general | solution.py:107
  41.8 1.0 %copy.33 = bf16[2,2,512,256]{3,2,1,0:T(8,128)(2,1)} copy(bf16[2,2,512,256]{3,2,0,1:T(8,128)(2,1)S(1)} %pad_maximum_fusion) | data formatting | bytes 2097152 | tf_op jit(solution)/shard_map/stack | solution.py:137
  (156 shorter events, 14.3 us)
Async XLA Ops:
  0.0 17.6 %copy-start.1 = (s32[2,2,32]{2,1,0:T(2,128)S(1)}, s32[2,2,32]{2,1,0:T(2,128)}, u32[]{:S(2)}) copy-start(s32[2,2,32]{2,1,0:T(2,128)} %param.22) | copy-start | bytes 1540
  0.0 18.3 %copy-start = (bf16[2,2,64,64]{3,2,1,0:T(8,128)(2,1)S(1)}, bf16[2,2,64,64]{3,2,1,0:T(8,128)(2,1)}, u32[]{:S(2)}) copy-start(bf16[2,2,64,64]{3,2,1,0:T(8,128)(2,1)} %param.20) | copy-start | bytes 98308
  1.9 18.8 %all-to-all-start = ((bf16[2,1,8,16,2,256]{5,4,2,0,1,3:T(2,128)(2,1)}), bf16[2,1,8,16,2,256]{5,4,2,0,1,3:T(2,128)(2,1)S(1)}, u32[]{:S(2)}, u32[]{:S(2)}) async-start(bf16[2,1,8,16,2,256]{5,4,2,0,1,3:T(2,128)(2,1)} %bitcast.76), calls=%async_computation | async-start | bytes 524288 | tf_op jit(solution)/shard_map/all_to_all | solution.py:75
where the time goes:
time: 43.2 us; the launch traced here: 42.8 us
  matrix products  15 us (35%)
  local copies, waits for them, and re-layouts  9.99 us (23%)
  other arithmetic  8.13 us (19%)
  starting transfers between devices  5.38 us (12%)
  between operations  2.9 us (7%)
  loops' own time  1.45 us (3%)
    dot_general x32, matrix products, sweep(): jnp.dot(misfit, operator, preferred_element_type=jnp.float32)  12.6 us
    all_to_all x1, starting transfers between devices, shards(): lax.all_to_all(image_stack.reshape(halves, 1, acq_share, azb_all, range_l...  5.38 us
    unnamed x5, local copies, waits for them, and re-layouts  1.93 us
    another operation x5, other arithmetic  1.82 us
    scatter x2, local copies, waits for them, and re-layouts, pack_order(): jnp.zeros_like(lane_slot).at[lane_slot]  1.55 us
    reduce_sum x2, other arithmetic, pack_order(): live_total = jnp.sum(live_flags)  1.48 us
    gather x2, local copies, waits for them, and re-layouts, solve_lanes(): return jnp.take(result, lane_slot, axis=0)  1.4 us
    slice x1, local copies, waits for them, and re-layouts, shards(): range_group[column] - first_group  1.34 us
  transfers between devices with their start and end apart: 1, of which 0 were waited for; matrix products, arithmetic and copies ran while one was open for 25% of the time, Pallas kernels for 0%

commit v1 on v0

--- a/solution.py
+++ b/solution.py
@@ -72,13 +72,19 @@
 
 def shards(image_stack, steering, wiener_filter, range_group, lay_list, lay_count):
     halves, acq_share, azb_all, range_local, block_pixels = image_stack.shape
-    relaid = lax.all_to_all(
-        image_stack.reshape(halves, 1, acq_share, azb_all, range_local, block_pixels),
-        ("az", "acq"),
-        split_axis=3,
-        concat_axis=1,
-        tiled=True,
-    )
+    shard = image_stack.reshape(halves, 1, acq_share, azb_all, range_local, block_pixels)
+    ways, here = (lax.axis_size(("az", "acq")), lax.axis_index(("az", "acq")))
+    width = shard.shape[3] // ways
+    shape = list(shard.shape)
+    shape[3] = width
+    height = shape[1]
+    shape[1] = height * ways
+    relaid = jnp.zeros(shape, shard.dtype)
+    for mask in range(ways):
+        part = lax.dynamic_slice_in_dim(shard, (here ^ mask) * width, width, axis=3)
+        if mask:
+            part = lax.ppermute(part, ("az", "acq"), [(d, d ^ mask) for d in range(ways)])
+        relaid = lax.dynamic_update_slice_in_dim(relaid, part, (here ^ mask) * height, axis=1)
     blocks = lay_list.shape[0]
     pixels = relaid.reshape(2 * K, blocks, range_local, block_pixels)
     first_group = lax.axis_index("rg") * GRP_DEV

time: 43.2 us -> 48.3 us (1.12)
  starting transfers between devices: 5.38 us -> 8.75 us
  waiting for transfers between devices: 0.01 us -> 1.96 us
  local copies, waits for them, and re-layouts: 9.99 us -> 9.23 us
    ppermute x0 -> x7, starting transfers between devices: none -> 8.75 us  [shards(): lax.ppermute(part, ('az', 'acq'), [(d, d ^ mask) for d in range(ways)])]
    all_to_all x1 -> x0, starting transfers between devices: 5.38 us -> none  [shards(): lax.all_to_all(image_stack.reshape(halves, 1, acq_share, azb_all, range_l...]
    ppermute x0 -> x7, waiting for transfers between devices: none -> 1.96 us  [shards(): lax.ppermute(part, ('az', 'acq'), [(d, d ^ mask) for d in range(ways)])]
    unnamed x5 -> x11, local copies, waits for them, and re-layouts: 1.93 us -> 0.05 us
    another operation x2 -> x3, local copies, waits for them, and re-layouts: 0.01 us -> 1.12 us
    another operation x5 -> x6, other arithmetic: 1.82 us -> 1.91 us
  transfers between devices with their start and end apart: 1 -> 7, of which waited for: 0 -> 2; matrix products, arithmetic and copies ran while one was open for 25% -> 23% of each run, Pallas kernels for 0% -> 0%
where the time goes in v1:
time: 48.3 us; the launch traced here: 47.7 us
  matrix products  15.1 us (31%)
  local copies, waits for them, and re-layouts  9.23 us (19%)
  starting transfers between devices  8.75 us (18%)
  other arithmetic  8.22 us (17%)
  between operations  3.09 us (6%)
  waiting for transfers between devices  1.96 us (4%)
  loops' own time  1.42 us (3%)
    dot_general x32, matrix products, sweep(): jnp.dot(misfit, operator, preferred_element_type=jnp.float32)  12.6 us
    ppermute x7, starting transfers between devices, shards(): lax.ppermute(part, ('az', 'acq'), [(d, d ^ mask) for d in range(ways)])  8.75 us
    ppermute x7, waiting for transfers between devices, shards(): lax.ppermute(part, ('az', 'acq'), [(d, d ^ mask) for d in range(ways)])  1.96 us
    another operation x6, other arithmetic  1.91 us
    scatter x2, local copies, waits for them, and re-layouts, pack_order(): jnp.zeros_like(lane_slot).at[lane_slot]  1.55 us
    reduce_sum x2, other arithmetic, pack_order(): live_total = jnp.sum(live_flags)  1.48 us
    gather x2, local copies, waits for them, and re-layouts, solve_lanes(): return jnp.take(result, lane_slot, axis=0)  1.4 us
    dot_general x2, matrix products, shards(): jnp.einsum('ie,iap->aep', operator, filtered, preferred_element_type=jnp....  1.34 us
  transfers between devices with their start and end apart: 7, of which 2 were waited for; matrix products, arithmetic and copies ran while one was open for 23% of the time, Pallas kernels for 0%

profile of v1, /device:TPU:27, one launch (start us, length us, event | category | flops | bytes accessed | tf_op | source)
XLA Modules:
  0.0 47.7 jit_solution(13416366937161482213)
XLA Ops:
  0.0 1.1 %constant_dynamic-slice_fusion = (bf16[2,8,2,2,256]{4,3,2,1,0:T(2,128)(2,1)S(1)}, bf16[2,8,2,2,256]{4,3,2,1,0:T(2,128)(2,1)S(1)}, bf16[2,8,2,2,256]{4,3,2,1,0:T(...) fusion(bf16[2,8,16,2,256]{4,3,2,1,0:T(2,128)(2,1)} %param.18, ...), kind=kLoop, calls=%fused_computation.143 | loop fusion | bytes 524320 | tf_op jit(solution)/shard_map/dynamic-slice.7
  1.1 0.7 %collective-permute-start = (bf16[2,1,8,2,2,256]{5,2,4,3,1,0:T(8,128)(2,1)S(1)}, bf16[2,1,8,2,2,256]{5,2,4,3,1,0:T(8,128)(2,1)S(1)}, u32[]{:S(2)}, u32[]{:S(2)}) collective-permute-start(bf16[2,1,8,2,2,256]{5,2,4,3,1,0:T(8,128)(2,1)S(1)} %bitcast.115), channel_id=1, source_target_pairs={{0,1},{1,0},{4,5},{5,4},{8,9},{9,8},{12,13},{13,12},{2,3},{3,2},{6... | collective-permute-start | bytes 98312 | tf_op jit(solution)/shard_map/ppermute | solution.py:86
  2.1 1.5 %collective-permute-start.2 = (bf16[2,1,8,2,2,256]{5,2,4,3,1,0:T(8,128)(2,1)S(1)}, bf16[2,1,8,2,2,256]{5,2,4,3,1,0:T(8,128)(2,1)S(1)}, u32[]{:S(2)}, u32[]{:S(2)}) collective-permute-start(bf16[2,1,8,2,2,256]{5,2,4,3,1,0:T(8,128)(2,1)S(1)} %bitcast.113), channel_id=1, source_target_pairs={{0,5},{1,4},{4,1},{5,0},{8,13},{9,12},{12,9},{13,8},{2,7},{3,6},{6... | collective-permute-start | bytes 98312 | tf_op jit(solution)/shard_map/ppermute | solution.py:86
  3.7 2.6 %collective-permute-start.4 = (bf16[2,1,8,2,2,256]{5,2,4,3,1,0:T(8,128)(2,1)S(1)}, bf16[2,1,8,2,2,256]{5,2,4,3,1,0:T(8,128)(2,1)S(1)}, u32[]{:S(2)}, u32[]{:S(2)}) collective-permute-start(bf16[2,1,8,2,2,256]{5,2,4,3,1,0:T(8,128)(2,1)S(1)} %bitcast.111), channel_id=1, source_target_pairs={{0,9},{1,8},{4,13},{5,12},{8,1},{9,0},{12,5},{13,4},{2,11},{3,10},... | collective-permute-start | bytes 98312 | tf_op jit(solution)/shard_map/ppermute | solution.py:86
  6.3 1.0 %slice_reduce_fusion.1 = (s32[2]{0:T(128)S(1)}, s32[2]{0:T(128)S(1)}) fusion(s32[2,2]{1,0:T(2,128)} %param.23), kind=kLoop, calls=%fused_computation.165 | loop fusion | bytes 32 | tf_op jit(solution)/shard_map/slice | solution.py:116
  7.3 0.7 %convert_reduce_fusion.2 = s32[]{:T(128)} fusion(s32[2]{0:T(128)S(1)} %get-tuple-element.176), kind=kLoop, calls=%fused_computation.159 | loop fusion | flops 191 | bytes 12 | tf_op jit(solution)/shard_map/reduce_sum | solution.py:46
  8.4 0.8 %convert_reduce_fusion.3 = s32[]{:T(128)} fusion(s32[2]{0:T(128)S(1)} %get-tuple-element.175), kind=kLoop, calls=%fused_computation.162 | loop fusion | flops 191 | bytes 12 | tf_op jit(solution)/shard_map/reduce_sum | solution.py:46
  9.3 1.3 %fusion.95 = (s32[1]{0:T(128)}, s32[1]{0:T(128)}) fusion(s32[2]{0:T(128)} %param.21), kind=kLoop, calls=%fused_computation.182 | loop fusion | bytes 16 | tf_op jit(solution)/shard_map/slice | solution.py:97
  11.9 1.1 %select_reduce_fusion.1 = (bf16[2,64,512]{2,1,0:T(8,128)(2,1)S(1)}, bf16[2,64,512]{2,1,0:T(8,128)(2,1)S(1)}) fusion(bf16[2,2,64,512]{3,2,1,0:T(8,128)(2,1)} %param.19, pred[2]{0:T(512)(128)(4,1)S(1)} %iota_compare_fusion.5, pred[2]{0:T(512)(128)(4,1)S(1)} %iota_compare_fusion.4), kind=kLoop, calls=%fused_computation.70 | loop fusion | flops 393216 | bytes 524292 | tf_op jit(solution)/shard_map/reduce_sum | solution.py:98
  13.7 0.7 %fusion.93 = (s32[64]{0:T(128)S(1)}, s32[64]{0:T(128)S(1)}, s32[64]{0:T(128)S(1)}) fusion(s32[64,1]{1,0:T(8,128)S(1)} %reduce-window.16, pred[64,1]{1,0:T(8,128)(4,1)S(1)} %lt.225, s32[64,1]{1,0:T(8,128)S(1)} %reduce-window.19, s32[]{:T(128)} %convert_reduce_fusion.2), kind=kLoop, calls=%fused_computation.180 | loop fusion | flops 576 | bytes 1348 | tf_op jit(solution)/shard_map/reduce-window.2
  14.4 0.8 %scatter_custom_fusion.1 = s32[64]{0:T(128)S(1)} fusion(s32[64]{0:T(128)S(1)} %get-tuple-element.173, s32[64]{0:T(128)S(1)} %iota.37, s32[]{:T(128)} %constant.143.clone.1), kind=kCustom, calls=%fused_computation.169 | custom fusion | bytes 260 | tf_op jit(solution)/shard_map/scatter | solution.py:51
  15.2 0.8 %fusion.92 = (s32[64]{0:T(128)S(1)}, s32[64]{0:T(128)S(1)}, s32[64]{0:T(128)S(1)}) fusion(s32[64,1]{1,0:T(8,128)S(1)} %reduce-window.14, pred[64,1]{1,0:T(8,128)(4,1)S(1)} %lt.224, s32[64,1]{1,0:T(8,128)S(1)} %reduce-window.15, s32[]{:T(128)} %convert_reduce_fusion.3), kind=kLoop, calls=%fused_computation.179 | loop fusion | flops 576 | bytes 1348 | tf_op jit(solution)/shard_map/reduce-window
  16.0 0.8 %scatter_custom_fusion = s32[64]{0:T(128)S(1)} fusion(s32[64]{0:T(128)S(1)} %get-tuple-element.170, s32[64]{0:T(128)S(1)} %iota.35, s32[]{:T(128)} %constant.143.clone.1), kind=kCustom, calls=%fused_computation.171 | custom fusion | bytes 260 | tf_op jit(solution)/shard_map/scatter | solution.py:51
  16.8 0.6 %compare_and_fusion = (pred[64]{0:T(512)(128)(4,1)S(1)}, s32[64]{0:T(128)S(1)}, pred[64]{0:T(512)(128)(4,1)S(1)}) fusion(pred[64]{0:T(512)(128)(4,1)S(1)} %lt.209, s32[64]{0:T(128)S(1)} %get-tuple-element.174, s32[]{:T(128)} %convert_reduce_fusion.2, s32[64]{0:T(128)S(1)} %get-tuple-element.172, s32[64]{0:T(128)S(1)} %scatter_custom_fusion.1), kind=kLoop, calls=%fused_computation.155 | loop fusion | flops 1152 | bytes 1220 | tf_op jit(solution)/shard_map/jit(_take)/and | solution.py:70
  17.7 0.7 %compare_and_fusion.2 = (pred[64]{0:T(512)(128)(4,1)S(1)}, s32[64]{0:T(128)S(1)}, pred[64]{0:T(512)(128)(4,1)S(1)}) fusion(pred[64]{0:T(512)(128)(4,1)S(1)} %lt.203, s32[64]{0:T(128)S(1)} %get-tuple-element.171, s32[]{:T(128)} %convert_reduce_fusion.3, s32[64]{0:T(128)S(1)} %get-tuple-element.169, s32[64]{0:T(128)S(1)} %scatter_custom_fusion), kind=kLoop, calls=%fused_computation.157 | loop fusion | flops 1152 | bytes 1220 | tf_op jit(solution)/shard_map/jit(_take)/and | solution.py:70
  20.0 3.5 %collective-permute-start.6 = (bf16[2,1,8,2,2,256]{5,2,4,3,1,0:T(8,128)(2,1)S(1)}, bf16[2,1,8,2,2,256]{5,2,4,3,1,0:T(8,128)(2,1)S(1)}, u32[]{:S(2)}, u32[]{:S(2)}) collective-permute-start(bf16[2,1,8,2,2,256]{5,2,4,3,1,0:T(8,128)(2,1)S(1)} %bitcast.116), channel_id=1, source_target_pairs={{0,13},{1,12},{4,9},{5,8},{8,5},{9,4},{12,1},{13,0},{2,15},{3,14},... | collective-permute-start | bytes 98312 | tf_op jit(solution)/shard_map/ppermute | solution.py:86
  23.6 0.9 %collective-permute-done.5 = bf16[2,1,8,2,2,256]{5,2,4,3,1,0:T(8,128)(2,1)S(1)} collective-permute-done((bf16[2,1,8,2,2,256]{5,2,4,3,1,0:T(8,128)(2,1)S(1)}, bf16[2,1,8,2,2,256]{5,2,4,3,1,0:T(8,128)(2,1)S(1)}, u32[]{:S(2)}, u32[]{:S(2)}) %collective-permute-start.5) | collective-permute-done | bytes 32800 | tf_op jit(solution)/shard_map/ppermute | solution.py:86
  24.5 1.0 %collective-permute-done.6 = bf16[2,1,8,2,2,256]{5,2,4,3,1,0:T(8,128)(2,1)S(1)} collective-permute-done((bf16[2,1,8,2,2,256]{5,2,4,3,1,0:T(8,128)(2,1)S(1)}, bf16[2,1,8,2,2,256]{5,2,4,3,1,0:T(8,128)(2,1)S(1)}, u32[]{:S(2)}, u32[]{:S(2)}) %collective-permute-start.6) | collective-permute-done | bytes 32800 | tf_op jit(solution)/shard_map/ppermute | solution.py:86
  26.0 0.6 %gather_fusion.2 = bf16[64,128]{1,0:T(8,128)(2,1)S(1)} fusion(bf16[64,128]{1,0:T(8,128)(2,1)S(1)} %bitcast.108, s32[1024]{0:T(1024)S(1)} %pad_clamp_fusion.1), kind=kCustom, calls=%fused_computation.2.clone | custom fusion | bytes 33024 | tf_op jit(solution)/shard_map/jit(_take)/gather | solution.py:58
  26.7 7.7 %while.49 = (s32[]{:T(128)}, bf16[64,512]{1,0:T(8,128)(2,1)S(1)}, s32[]{:T(128)}, bf16[64,128]{1,0:T(8,128)(2,1)S(1)}, bf16[128,1024]{1,0:T(8,128)(2,1)S(1)}, /*...) while((s32[]{:T(128)}, bf16[64,512]{1,0:T(8,128)(2,1)S(1)}, ...), condition=%wide.region_20.23_spmd, body=%wide.region_17.22_spmd.sunk | while | flops 17199112 | bytes 1253690 | solution.py:69
  26.8 3.8 %while.51 = (s32[]{:T(128)}, f32[32,1024]{1,0:T(8,128)S(1)}, bf16[128,1024]{1,0:T(8,128)(2,1)S(1)}, f32[32,128]{1,0:T(8,128)S(1)}, s32[]{:T(128)}, /*index=5*/s32[]{:T(128)}) while((s32[]{:T(128)}, f32[32,1024]{1,0:T(8,128)S(1)}, bf16[128,1024]{1,0:T(8,128)(2,1)S(1)}, f32[32,128]{1,0:T(8,128)S(1)}, s32[]{:T(128)}, ...), condition=%wide.region_19.21_spmd.clone, body=%wide.region_18.20_spmd.clone.sunk | while | flops 17129476 | bytes 1065047 | solution.py:40
  26.8 0.4 fusion.116
  30.6 3.8 %while.51 = (s32[]{:T(128)}, f32[32,1024]{1,0:T(8,128)S(1)}, bf16[128,1024]{1,0:T(8,128)(2,1)S(1)}, f32[32,128]{1,0:T(8,128)S(1)}, s32[]{:T(128)}, /*index=5*/s32[]{:T(128)}) while((s32[]{:T(128)}, f32[32,1024]{1,0:T(8,128)S(1)}, bf16[128,1024]{1,0:T(8,128)(2,1)S(1)}, f32[32,128]{1,0:T(8,128)S(1)}, s32[]{:T(128)}, ...), condition=%wide.region_19.21_spmd.clone, body=%wide.region_18.20_spmd.clone.sunk | while | flops 17129476 | bytes 1065047 | solution.py:40
  34.4 0.6 %gather_fusion = bf16[64,128]{1,0:T(8,128)(2,1)S(1)} fusion(bf16[64,128]{1,0:T(8,128)(2,1)S(1)} %bitcast.107, s32[1024]{0:T(1024)S(1)} %pad_clamp_fusion.3), kind=kCustom, calls=%fused_computation.clone | custom fusion | bytes 33024 | tf_op jit(solution)/shard_map/jit(_take)/gather | solution.py:58
  35.2 7.7 %while.47 = (s32[]{:T(128)}, bf16[64,512]{1,0:T(8,128)(2,1)S(1)}, s32[]{:T(128)}, bf16[64,128]{1,0:T(8,128)(2,1)S(1)}, bf16[128,1024]{1,0:T(8,128)(2,1)S(1)}, /*...) while((s32[]{:T(128)}, bf16[64,512]{1,0:T(8,128)(2,1)S(1)}, ...), condition=%wide.region_9.11_spmd, body=%wide.region_6.10_spmd.sunk | while | flops 17199112 | bytes 1253690 | solution.py:69
  35.2 3.8 %while.50 = (s32[]{:T(128)}, f32[32,1024]{1,0:T(8,128)S(1)}, bf16[128,1024]{1,0:T(8,128)(2,1)S(1)}, f32[32,128]{1,0:T(8,128)S(1)}, s32[]{:T(128)}, /*index=5*/s32[]{:T(128)}) while((s32[]{:T(128)}, f32[32,1024]{1,0:T(8,128)S(1)}, bf16[128,1024]{1,0:T(8,128)(2,1)S(1)}, f32[32,128]{1,0:T(8,128)S(1)}, s32[]{:T(128)}, ...), condition=%wide.region_8.9_spmd.clone, body=%wide.region_7.8_spmd.clone.sunk | while | flops 17129476 | bytes 1065047 | solution.py:40
  39.1 3.8 %while.50 = (s32[]{:T(128)}, f32[32,1024]{1,0:T(8,128)S(1)}, bf16[128,1024]{1,0:T(8,128)(2,1)S(1)}, f32[32,128]{1,0:T(8,128)S(1)}, s32[]{:T(128)}, /*index=5*/s32[]{:T(128)}) while((s32[]{:T(128)}, f32[32,1024]{1,0:T(8,128)S(1)}, bf16[128,1024]{1,0:T(8,128)(2,1)S(1)}, f32[32,128]{1,0:T(8,128)S(1)}, s32[]{:T(128)}, ...), condition=%wide.region_8.9_spmd.clone, body=%wide.region_7.8_spmd.clone.sunk | while | flops 17129476 | bytes 1065047 | solution.py:40
  42.9 0.7 %gather_fusion.3 = bf16[64,512]{1,0:T(8,128)(2,1)S(1)} fusion(bf16[64,512]{1,0:T(8,128)(2,1)S(1)} %get-tuple-element.134, s32[1024]{0:T(1024)S(1)} %pad_clamp_fusion), kind=kCustom, calls=%fused_computation.3.clone | custom fusion | bytes 131328 | tf_op jit(solution)/shard_map/jit(_take)/gather | solution.py:70
  43.7 0.7 %gather_fusion.1 = bf16[64,512]{1,0:T(8,128)(2,1)S(1)} fusion(bf16[64,512]{1,0:T(8,128)(2,1)S(1)} %get-tuple-element.133, s32[1024]{0:T(1024)S(1)} %pad_clamp_fusion.2), kind=kCustom, calls=%fused_computation.1.clone | custom fusion | bytes 131328 | tf_op jit(solution)/shard_map/jit(_take)/gather | solution.py:70
  44.5 0.7 %convolution_bitcast_fusion = f32[2,1024,256]{2,1,0:T(8,128)S(1)} fusion(bf16[128,2,2,256]{3,0,1,2:T(8,128)(2,1)S(1)} %bitcast.105, bf16[64,64]{1,0:T(8,128)(2,1)S(1)} %get-tuple-element.232, bf16[64,64]{1,0:T(8,128)(2,1)S(1)} %get-tuple-element.231, bf16[64,64]{1,0:T(8,128)(2,1)S(1)} %get-tuple-element.248, bf16[64,512]{1,0:T(8,128)(2,1)S(1)} %get-tuple-element.228, ...), kind=kOutput, calls=%fused_computation.46 | convolution fusion | flops 152240128 | bytes 2473984 | tf_op jit(solution)/shard_map/ie,iap->aep/dot_general | solution.py:113
  45.5 0.7 %convolution_bitcast_fusion.1 = f32[2,1024,256]{2,1,0:T(8,128)S(1)} fusion(bf16[128,2,2,256]{3,0,1,2:T(8,128)(2,1)S(1)} %bitcast.106, bf16[64,64]{1,0:T(8,128)(2,1)S(1)} %get-tuple-element.245, bf16[64,64]{1,0:T(8,128)(2,1)S(1)} %get-tuple-element.246, bf16[64,64]{1,0:T(8,128)(2,1)S(1)} %get-tuple-element.247, bf16[64,512]{1,0:T(8,128)(2,1)S(1)} %get-tuple-element.241, ...), kind=kOutput, calls=%fused_computation.47 | convolution fusion | flops 152240128 | bytes 2473984 | tf_op jit(solution)/shard_map/ie,iap->aep/dot_general | solution.py:113
  46.7 1.0 %copy.36 = bf16[2,2,512,256]{3,2,1,0:T(8,128)(2,1)} copy(bf16[2,2,512,256]{3,2,0,1:T(8,128)(2,1)S(1)} %pad_maximum_fusion) | data formatting | bytes 2097152 | tf_op jit(solution)/shard_map/stack | solution.py:143
  (181 shorter events, 17.0 us)
Async XLA Ops:
  0.0 13.1 %copy-start = (bf16[2,2,64,64]{3,2,1,0:T(8,128)(2,1)S(1)}, bf16[2,2,64,64]{3,2,1,0:T(8,128)(2,1)}, u32[]{:S(2)}) copy-start(bf16[2,2,64,64]{3,2,1,0:T(8,128)(2,1)} %param.20) | copy-start | bytes 98308
  0.0 13.3 %copy-start.1 = (s32[2,2,32]{2,1,0:T(2,128)S(1)}, s32[2,2,32]{2,1,0:T(2,128)}, u32[]{:S(2)}) copy-start(s32[2,2,32]{2,1,0:T(2,128)} %param.22) | copy-start | bytes 1540
  1.1 18.8 %collective-permute-start = (bf16[2,1,8,2,2,256]{5,2,4,3,1,0:T(8,128)(2,1)S(1)}, bf16[2,1,8,2,2,256]{5,2,4,3,1,0:T(8,128)(2,1)S(1)}, u32[]{:S(2)}, u32[]{:S(2)}) collective-permute-start(bf16[2,1,8,2,2,256]{5,2,4,3,1,0:T(8,128)(2,1)S(1)} %bitcast.115), channel_id=1, source_target_pairs={{0,1},{1,0},{4,5},{5,4},{8,9},{9,8},{12,13},{13,12},{2,3},{3,2},{6... | collective-permute-start | bytes 98312 | tf_op jit(solution)/shard_map/ppermute | solution.py:86
  1.9 18.1 %collective-permute-start.1 = (bf16[2,1,8,2,2,256]{5,2,4,3,1,0:T(8,128)(2,1)S(1)}, bf16[2,1,8,2,2,256]{5,2,4,3,1,0:T(8,128)(2,1)S(1)}, u32[]{:S(2)}, u32[]{:S(2)}) collective-permute-start(bf16[2,1,8,2,2,256]{5,2,4,3,1,0:T(8,128)(2,1)S(1)} %bitcast.114), channel_id=1, source_target_pairs={{0,4},{1,5},{4,0},{5,1},{8,12},{9,13},{12,8},{13,9},{2,6},{3,7},{6... | collective-permute-start | bytes 98312 | tf_op jit(solution)/shard_map/ppermute | solution.py:86
  2.1 21.5 %collective-permute-start.2 = (bf16[2,1,8,2,2,256]{5,2,4,3,1,0:T(8,128)(2,1)S(1)}, bf16[2,1,8,2,2,256]{5,2,4,3,1,0:T(8,128)(2,1)S(1)}, u32[]{:S(2)}, u32[]{:S(2)}) collective-permute-start(bf16[2,1,8,2,2,256]{5,2,4,3,1,0:T(8,128)(2,1)S(1)} %bitcast.113), channel_id=1, source_target_pairs={{0,5},{1,4},{4,1},{5,0},{8,13},{9,12},{12,9},{13,8},{2,7},{3,6},{6... | collective-permute-start | bytes 98312 | tf_op jit(solution)/shard_map/ppermute | solution.py:86
  3.6 20.0 %collective-permute-start.3 = (bf16[2,1,8,2,2,256]{5,2,4,3,1,0:T(8,128)(2,1)S(1)}, bf16[2,1,8,2,2,256]{5,2,4,3,1,0:T(8,128)(2,1)S(1)}, u32[]{:S(2)}, u32[]{:S(2)}) collective-permute-start(bf16[2,1,8,2,2,256]{5,2,4,3,1,0:T(8,128)(2,1)S(1)} %bitcast.112), channel_id=1, source_target_pairs={{0,8},{1,9},{4,12},{5,13},{8,0},{9,1},{12,4},{13,5},{2,10},{3,11},... | collective-permute-start | bytes 98312 | tf_op jit(solution)/shard_map/ppermute | solution.py:86
  3.7 19.9 %collective-permute-start.4 = (bf16[2,1,8,2,2,256]{5,2,4,3,1,0:T(8,128)(2,1)S(1)}, bf16[2,1,8,2,2,256]{5,2,4,3,1,0:T(8,128)(2,1)S(1)}, u32[]{:S(2)}, u32[]{:S(2)}) collective-permute-start(bf16[2,1,8,2,2,256]{5,2,4,3,1,0:T(8,128)(2,1)S(1)} %bitcast.111), channel_id=1, source_target_pairs={{0,9},{1,8},{4,13},{5,12},{8,1},{9,0},{12,5},{13,4},{2,11},{3,10},... | collective-permute-start | bytes 98312 | tf_op jit(solution)/shard_map/ppermute | solution.py:86
  19.9 4.6 %collective-permute-start.5 = (bf16[2,1,8,2,2,256]{5,2,4,3,1,0:T(8,128)(2,1)S(1)}, bf16[2,1,8,2,2,256]{5,2,4,3,1,0:T(8,128)(2,1)S(1)}, u32[]{:S(2)}, u32[]{:S(2)}) collective-permute-start(bf16[2,1,8,2,2,256]{5,2,4,3,1,0:T(8,128)(2,1)S(1)} %bitcast.117), channel_id=1, source_target_pairs={{0,12},{1,13},{4,8},{5,9},{8,4},{9,5},{12,0},{13,1},{2,14},{3,15},... | collective-permute-start | bytes 98312 | tf_op jit(solution)/shard_map/ppermute | solution.py:86
  20.0 5.6 %collective-permute-start.6 = (bf16[2,1,8,2,2,256]{5,2,4,3,1,0:T(8,128)(2,1)S(1)}, bf16[2,1,8,2,2,256]{5,2,4,3,1,0:T(8,128)(2,1)S(1)}, u32[]{:S(2)}, u32[]{:S(2)}) collective-permute-start(bf16[2,1,8,2,2,256]{5,2,4,3,1,0:T(8,128)(2,1)S(1)} %bitcast.116), channel_id=1, source_target_pairs={{0,13},{1,12},{4,9},{5,8},{8,5},{9,4},{12,1},{13,0},{2,15},{3,14},... | collective-permute-start | bytes 98312 | tf_op jit(solution)/shard_map/ppermute | solution.py:86
